TPU v7x, 32 devices: a whole 2x2x4 slice. The times are simulated.
32 devices in a mesh: data: 32 (over z, y, x, core).
Axes of the slice: x: 2, y: 2, z: 4, core: 2. Of those that a mesh axis runs over, the one named last changes fastest.
Arguments:
- grad_qkv: bfloat16 [32, 1, 3551232], P('data')
- weight_qkv: float32 [1, 3551232], P(None, 'data')
- mom_qkv: float32 [1, 3551232], P(None, 'data')
- var_qkv: float32 [1, 3551232], P(None, 'data')
- grad_proj: bfloat16 [32, 1, 1183744], P('data')
- weight_proj: float32 [1, 1183744], P(None, 'data')
- mom_proj: float32 [1, 1183744], P(None, 'data')
- var_proj: float32 [1, 1183744], P(None, 'data')
- grad_fc_in: bfloat16 [32, 1, 4734976], P('data')
- weight_fc_in: float32 [1, 4734976], P(None, 'data')
- mom_fc_in: float32 [1, 4734976], P(None, 'data')
- var_fc_in: float32 [1, 4734976], P(None, 'data')
- grad_fc_out: bfloat16 [32, 1, 4734976], P('data')
- weight_fc_out: float32 [1, 4734976], P(None, 'data')
- mom_fc_out: float32 [1, 4734976], P(None, 'data')
- var_fc_out: float32 [1, 4734976], P(None, 'data')
Outputs:
- output 1: bfloat16 [1, 3551232], replicated
- output 2: float32 [1, 3551232], P(None, 'data')
- output 3: float32 [1, 3551232], P(None, 'data')
- output 4: float32 [1, 3551232], P(None, 'data')
- output 5: bfloat16 [1, 1183744], replicated
- output 6: float32 [1, 1183744], P(None, 'data')
- output 7: float32 [1, 1183744], P(None, 'data')
- output 8: float32 [1, 1183744], P(None, 'data')
- output 9: bfloat16 [1, 4734976], replicated
- output 10: float32 [1, 4734976], P(None, 'data')
- output 11: float32 [1, 4734976], P(None, 'data')
- output 12: float32 [1, 4734976], P(None, 'data')
- output 13: bfloat16 [1, 4734976], replicated
- output 14: float32 [1, 4734976], P(None, 'data')
- output 15: float32 [1, 4734976], P(None, 'data')
- output 16: float32 [1, 4734976], P(None, 'data')
All inputs are finite; a program needn't handle non-finite values.
Results may differ from a plain program's by a relative error of at most 0.001.
Values are sent between devices in bfloat16 or wider.
A program may use at most 1 GiB of HBM per device.

v0:
```python
import jax
import jax.numpy as jnp
from jax import lax
from jax.sharding import PartitionSpec as P

STEP = 10
LEARN_RATE = 0.1
BETA_ONE = 0.9
BETA_TWO = 0.999
EPSILON = 1e-6
WEIGHT_DECAY = 0.01


def solution(mesh):
    groups = mesh.shape["data"]
    grad_spec = P("data", None, None)
    shard_spec = P(None, "data")
    full_spec = P(None, None)

    def lamb_tensor(local_grad, weight, first_mom, second_mom):
        layers = local_grad.shape[1]
        pieces = local_grad.reshape(layers, groups, local_grad.shape[2] // groups)
        received = lax.all_to_all(pieces, "data", 1, 1, tiled=True)
        grad_mean = jnp.sum(received, axis=1, dtype=jnp.float32) / groups
        new_first = BETA_ONE * first_mom + (1.0 - BETA_ONE) * grad_mean
        new_second = BETA_TWO * second_mom + (1.0 - BETA_TWO) * grad_mean * grad_mean
        direction = (new_first / (1.0 - BETA_ONE ** STEP)) / (jnp.sqrt(new_second / (1.0 - BETA_TWO ** STEP)) + EPSILON) + WEIGHT_DECAY * weight
        part_sums = jnp.stack([jnp.sum(weight * weight, axis=1), jnp.sum(direction * direction, axis=1)])
        norm_pair = jnp.sqrt(lax.psum(part_sums, "data"))
        trust_ratio = (norm_pair[0] / norm_pair[1])[:, None]
        new_weight = weight - LEARN_RATE * trust_ratio * direction
        replica = lax.all_gather(new_weight.astype(jnp.bfloat16), "data", axis=1, tiled=True)
        return replica, new_weight, new_first, new_second

    def device_step(*blocks):
        results = []
        for kind_pos in range(len(blocks) // 4):
            first_pos = 4 * kind_pos
            results.extend(lamb_tensor(blocks[first_pos], blocks[first_pos + 1], blocks[first_pos + 2], blocks[first_pos + 3]))
        return tuple(results)

    return jax.shard_map(device_step, mesh=mesh, in_specs=(grad_spec, shard_spec, shard_spec, shard_spec) * 4, out_specs=(full_spec, shard_spec, shard_spec, shard_spec) * 4, check_vma=False)
```

profile of v0, /device:TPU:0, one launch (start us, length us, event | category | flops | bytes accessed | tf_op | source)
XLA Modules:
  0.0 1395.3 jit_solution(963465474196378441)
XLA Ops:
  7.2 0.5 broadcast.197
  7.7 50.1 %reduce.13 = bf16[32,36992]{1,0:T(8,128)(2,1)S(1)} reduce(bf16[32,1,36992]{2,1,0:T(2,128)(2,1)} %bitcast.33, bf16[]{:T(256)} %broadcast.197), dimensions={1}, to_apply=%bitcast.18.reduce_sub_computation | reduce | bytes 4734978
  57.8 2.9 reshape.234
  60.7 7.9 all-to-all-start.1
  68.5 130.5 %reduce.12 = bf16[32,110976]{1,0:T(8,128)(2,1)} reduce(bf16[32,1,110976]{2,1,0:T(2,128)(2,1)} %bitcast.32, bf16[]{:T(256)} %broadcast.197), dimensions={1}, to_apply=%bitcast.16.reduce_sub_computation | reduce | bytes 14204930
  199.1 9.7 reshape.232
  208.8 0.0 all-to-all-done.1
  208.8 6.2 all-to-all-start
  215.0 156.8 %reduce.14 = bf16[32,147968]{1,0:T(8,128)(2,1)} reduce(bf16[32,1,147968]{2,1,0:T(2,128)(2,1)} %bitcast.28, bf16[]{:T(256)} %broadcast.197), dimensions={1}, to_apply=%bitcast.20.reduce_sub_computation | reduce | bytes 18939906
  371.8 8.4 reshape.236
  380.2 0.0 all-to-all-done
  380.2 6.3 all-to-all-start.2
  386.5 156.8 %reduce.15 = bf16[32,147968]{1,0:T(8,128)(2,1)} reduce(bf16[32,1,147968]{2,1,0:T(2,128)(2,1)} %bitcast.29, bf16[]{:T(256)} %broadcast.197), dimensions={1}, to_apply=%bitcast.22.reduce_sub_computation | reduce | bytes 18939906
  543.3 8.4 reshape.238
  551.7 33.6 %all-to-all-done.2 = bf16[32,2,73984]{2,1,0:T(2,128)(2,1)} async-done(((bf16[32,2,73984]{2,1,0:T(2,128)(2,1)}), bf16[32,2,73984]{2,1,0:T(2,128)(2,1)}, u32[]{:S(2)}, u32[]{:S(2)}) %all-to-all-start.2) | async-done | bytes 9469984 | tf_op jit(solution)/shard_map/all_to_all | solution.py:23
  585.3 12.6 all-to-all-start.3
  598.0 0.3 all-gather.7.cloned.1.call-start
  598.3 10.6 reshape.235
  608.8 7.5 convert_reduce_fusion.3
  616.4 2.4 multiply_reduce_fusion.6
  618.8 31.4 %reshape.233 = bf16[32,1,110976]{2,1,0:T(2,128)(2,1)} reshape(bf16[32,2,55488]{2,1,0:T(2,128)(2,1)} %all-to-all-done) | data formatting | bytes 14204928
  650.3 20.0 %convert_reduce_fusion.2 = f32[110976]{0:T(1024)S(1)} fusion(bf16[32,1,110976]{2,1,0:T(2,128)(2,1)} %reshape.233), kind=kLoop, calls=%fused_computation.2 | loop fusion | flops 6991488 | bytes 7546368 | tf_op jit(solution)/shard_map/reduce_sum | solution.py:24
  670.3 0.1 multiply_multiply_fusion.2
  670.4 4.8 multiply_reduce_fusion.4
  675.2 2.6 pad_maximum_fusion
  677.8 28.7 %reshape.237 = bf16[32,1,147968]{2,1,0:T(2,128)(2,1)} reshape(bf16[32,2,73984]{2,1,0:T(2,128)(2,1)} %all-to-all-done.2) | data formatting | bytes 18939904
  706.5 26.6 %convert_reduce_fusion.1 = f32[147968]{0:T(1024)S(1)} fusion(bf16[32,1,147968]{2,1,0:T(2,128)(2,1)} %reshape.237), kind=kLoop, calls=%fused_computation.1 | loop fusion | flops 9321984 | bytes 10061824 | tf_op jit(solution)/shard_map/reduce_sum | solution.py:24
  733.1 0.1 multiply_multiply_fusion.1
  733.2 63.6 %all-to-all-done.3 = bf16[32,2,73984]{2,1,0:T(2,128)(2,1)} async-done(((bf16[32,2,73984]{2,1,0:T(2,128)(2,1)}), bf16[32,2,73984]{2,1,0:T(2,128)(2,1)}, u32[]{:S(2)}, u32[]{:S(2)}) %all-to-all-start.3) | async-done | bytes 9469984 | tf_op jit(solution)/shard_map/all_to_all | solution.py:23
  796.8 28.7 %reshape.239 = bf16[32,1,147968]{2,1,0:T(2,128)(2,1)} reshape(bf16[32,2,73984]{2,1,0:T(2,128)(2,1)} %all-to-all-done.3) | data formatting | bytes 18939904
  825.5 0.0 copy-start.6
  825.5 0.0 copy-start.7
  825.6 26.5 %convert_reduce_fusion = f32[147968]{0:T(1024)S(1)} fusion(bf16[32,1,147968]{2,1,0:T(2,128)(2,1)} %reshape.239), kind=kLoop, calls=%fused_computation | loop fusion | flops 9321984 | bytes 10061824 | tf_op jit(solution)/shard_map/reduce_sum | solution.py:24
  852.0 0.1 multiply_multiply_fusion
  852.2 0.0 copy-done.2
  852.2 5.8 multiply_reduce_fusion.2
  858.0 5.8 multiply_reduce_fusion
  863.8 2.6 pad_maximum_fusion.2
  866.4 46.5 %all-reduce = (f32[2,1]{1,0:T(2,128)S(1)}, f32[2,1]{1,0:T(2,128)S(1)}, f32[2,1]{1,0:T(2,128)S(1)}, f32[2,1]{1,0:T(2,128)S(1)}) all-reduce(f32[2,1]{1,0:T(2,128)S(1)} %get-tuple-element.64, f32[2,1]{1,0:T(2,128)S(1)} %get-tuple-element.65, f32[2,1]{1,0:T(2,128)S(1)} %get-tuple-element.66, ...), channel_id=1, replica_groups=mesh['data'=32] {'data'}, use_global_device_ids=true, to_apply=%region_3.0 | all-reduce | flops 8 | bytes 64 | tf_op jit(solution)/shard_map/psum | solution.py:29
  912.9 0.5 fusion.6
  914.8 1.9 fusion.2
  916.7 0.0 all-gather.7.cloned.1.call-update
  916.7 0.0 all-gather.5.cloned.1.call-start
  916.8 0.5 fusion.7
  918.6 2.5 fusion.3
  921.2 0.5 fusion.4
  923.0 0.0 all-gather.5.cloned.1.call-update
  923.1 0.0 all-gather.11.cloned.1.call-start
  923.1 1.7 fusion
  924.8 0.5 fusion.5
  926.7 0.0 all-gather.11.cloned.1.call-update
  926.7 0.0 all-gather.9.cloned.1.call-start
  926.7 1.7 fusion.1
  928.4 0.0 all-gather.9.cloned.1.call-update
  928.4 52.7 %all-gather.7.cloned.1.call-done = bf16[1,1183744]{1,0:T(2,128)(2,1)} async-done(((bf16[1,36992]{1,0:T(2,128)(2,1)}), bf16[1,1183744]{1,0:T(2,128)(2,1)}) %all-gather.7.cloned.1.call-update) | async-done | bytes 2367504 | tf_op jit(solution)/shard_map/all_gather | solution.py:32
  981.1 105.2 %all-gather.5.cloned.1.call-done = bf16[1,3551232]{1,0:T(2,128)(2,1)} async-done(((bf16[1,110976]{1,0:T(2,128)(2,1)}), bf16[1,3551232]{1,0:T(2,128)(2,1)}) %all-gather.5.cloned.1.call-update) | async-done | bytes 7102480 | tf_op jit(solution)/shard_map/all_gather | solution.py:32
  1086.3 125.7 %all-gather.11.cloned.1.call-done = bf16[1,4734976]{1,0:T(2,128)(2,1)} async-done(((bf16[1,147968]{1,0:T(2,128)(2,1)}), bf16[1,4734976]{1,0:T(2,128)(2,1)}) %all-gather.11.cloned.1.call-update) | async-done | bytes 9469968 | tf_op jit(solution)/shard_map/all_gather | solution.py:32
  1212.0 125.8 %all-gather.9.cloned.1.call-done = bf16[1,4734976]{1,0:T(2,128)(2,1)} async-done(((bf16[1,147968]{1,0:T(2,128)(2,1)}), bf16[1,4734976]{1,0:T(2,128)(2,1)}) %all-gather.9.cloned.1.call-update) | async-done | bytes 9469968 | tf_op jit(solution)/shard_map/all_gather | solution.py:32
  1337.8 17.5 %copy.36 = bf16[1,3551232]{1,0:T(2,128)(2,1)} copy(bf16[1,3551232]{1,0:T(2,128)(2,1)} %all-gather.5.cloned.1.call-done) | data formatting | bytes 14204928
  1355.3 0.0 slice-start
  1355.3 0.0 slice-start.1
  1355.3 2.4 copy.37
  1357.7 23.6 %copy.38 = bf16[1,4734976]{1,0:T(2,128)(2,1)} copy(bf16[1,4734976]{1,0:T(2,128)(2,1)} %all-gather.9.cloned.1.call-done) | data formatting | bytes 18939904
  1381.4 6.9 copy.39
  (37 shorter events, 0.1 us)
Async XLA Ops:
  60.7 148.1 %all-to-all-start.1 = ((bf16[32,2,18496]{2,1,0:T(2,128)(2,1)}), bf16[32,2,18496]{2,1,0:T(2,128)(2,1)S(1)}, u32[]{:S(2)}, u32[]{:S(2)}) async-start(bf16[32,2,18496]{2,1,0:T(2,128)(2,1)} %reshape.234), calls=%async_computation.1 | async-start | bytes 4751360 | tf_op jit(solution)/shard_map/all_to_all | solution.py:23
  208.8 171.5 %all-to-all-start = ((bf16[32,2,55488]{2,1,0:T(2,128)(2,1)}), bf16[32,2,55488]{2,1,0:T(2,128)(2,1)}, u32[]{:S(2)}, u32[]{:S(2)}) async-start(bf16[32,2,55488]{2,1,0:T(2,128)(2,1)} %reshape.232), calls=%async_computation | async-start | bytes 14221312 | tf_op jit(solution)/shard_map/all_to_all | solution.py:23
  380.2 205.1 %all-to-all-start.2 = ((bf16[32,2,73984]{2,1,0:T(2,128)(2,1)}), bf16[32,2,73984]{2,1,0:T(2,128)(2,1)}, u32[]{:S(2)}, u32[]{:S(2)}) async-start(bf16[32,2,73984]{2,1,0:T(2,128)(2,1)} %reshape.236), calls=%async_computation.2 | async-start | bytes 18939904 | tf_op jit(solution)/shard_map/all_to_all | solution.py:23
  551.7 64.6 %copy-start.8 = (f32[1,36992]{1,0:T(1,128)S(1)}, f32[1,36992]{1,0:T(1,128)}, u32[]{:S(2)}) copy-start(f32[1,36992]{1,0:T(1,128)} %param.21) | copy-start | bytes 443908
  551.7 64.6 %copy-start.11 = (f32[1,36992]{1,0:T(1,128)S(1)}, f32[1,36992]{1,0:T(1,128)}, u32[]{:S(2)}) copy-start(f32[1,36992]{1,0:T(1,128)} %param.22) | copy-start | bytes 443908
  551.7 64.7 %copy-start.12 = (f32[1,36992]{1,0:T(1,128)S(1)}, f32[1,36992]{1,0:T(1,128)}, u32[]{:S(2)}) copy-start(f32[1,36992]{1,0:T(1,128)} %param.23) | copy-start | bytes 443908
  585.3 211.5 %all-to-all-start.3 = ((bf16[32,2,73984]{2,1,0:T(2,128)(2,1)}), bf16[32,2,73984]{2,1,0:T(2,128)(2,1)}, u32[]{:S(2)}, u32[]{:S(2)}) async-start(bf16[32,2,73984]{2,1,0:T(2,128)(2,1)} %reshape.238), calls=%async_computation.3 | async-start | bytes 18939904 | tf_op jit(solution)/shard_map/all_to_all | solution.py:23
  598.0 383.2 %all-gather.7.cloned.1.call-start = ((), (), s32[]{:S(2)}) async-start(), calls=%async_computation.5 | async-start | bytes 4882944 | tf_op jit(solution)/shard_map/all_gather | solution.py:32
  618.8 51.5 %copy-start.3 = (f32[1,110976]{1,0:T(1,128)S(1)}, f32[1,110976]{1,0:T(1,128)}, u32[]{:S(2)}) copy-start(f32[1,110976]{1,0:T(1,128)} %param.17) | copy-start | bytes 1331716
  618.8 51.5 %copy-start.9 = (f32[1,110976]{1,0:T(1,128)S(1)}, f32[1,110976]{1,0:T(1,128)}, u32[]{:S(2)}) copy-start(f32[1,110976]{1,0:T(1,128)} %param.18) | copy-start | bytes 1331716
  618.8 51.6 %copy-start.10 = (f32[1,110976]{1,0:T(1,128)S(1)}, f32[1,110976]{1,0:T(1,128)}, u32[]{:S(2)}) copy-start(f32[1,110976]{1,0:T(1,128)} %param.19) | copy-start | bytes 1331716
  825.5 26.6 %copy-start.2 = (f32[1,147968]{1,0:T(1,128)S(1)}, f32[1,147968]{1,0:T(1,128)}, u32[]{:S(2)}) copy-start(f32[1,147968]{1,0:T(1,128)} %param.25) | copy-start | bytes 1775620
  825.5 26.7 %copy-start.4 = (f32[1,147968]{1,0:T(1,128)S(1)}, f32[1,147968]{1,0:T(1,128)}, u32[]{:S(2)}) copy-start(f32[1,147968]{1,0:T(1,128)} %param.26) | copy-start | bytes 1775620
  825.5 26.7 %copy-start.5 = (f32[1,147968]{1,0:T(1,128)S(1)}, f32[1,147968]{1,0:T(1,128)}, u32[]{:S(2)}) copy-start(f32[1,147968]{1,0:T(1,128)} %param.27) | copy-start | bytes 1775620
  825.5 32.5 %copy-start.1 = (f32[1,147968]{1,0:T(1,128)S(1)}, f32[1,147968]{1,0:T(1,128)}, u32[]{:S(2)}) copy-start(f32[1,147968]{1,0:T(1,128)} %param.29) | copy-start | bytes 1775620
  825.5 32.5 %copy-start.6 = (f32[1,147968]{1,0:T(1,128)S(1)}, f32[1,147968]{1,0:T(1,128)}, u32[]{:S(2)}) copy-start(f32[1,147968]{1,0:T(1,128)} %param.30) | copy-start | bytes 1775620
  825.5 32.5 %copy-start.7 = (f32[1,147968]{1,0:T(1,128)S(1)}, f32[1,147968]{1,0:T(1,128)}, u32[]{:S(2)}) copy-start(f32[1,147968]{1,0:T(1,128)} %param.31) | copy-start | bytes 1775620
  916.7 169.6 %all-gather.5.cloned.1.call-start = ((), (), s32[]{:S(2)}) async-start(), calls=%async_computation.4 | async-start | bytes 14648832 | tf_op jit(solution)/shard_map/all_gather | solution.py:32
  923.1 289.0 %all-gather.11.cloned.1.call-start = ((), (), s32[]{:S(2)}) async-start(), calls=%async_computation.7 | async-start | bytes 19531776 | tf_op jit(solution)/shard_map/all_gather | solution.py:32
  926.7 411.1 %all-gather.9.cloned.1.call-start = ((), (), s32[]{:S(2)}) async-start(), calls=%async_computation.6 | async-start | bytes 19531776 | tf_op jit(solution)/shard_map/all_gather | solution.py:32
  1337.8 17.5 %copy-start = (bf16[1,1183744]{1,0:T(2,128)(2,1)S(1)}, bf16[1,1183744]{1,0:T(2,128)(2,1)}, u32[]{:S(2)}) copy-start(bf16[1,1183744]{1,0:T(2,128)(2,1)} %all-gather.7.cloned.1.call-done) | copy-start | bytes 7102468
  1355.3 26.0 %slice-start = ((s8[18939904]{0:T(1024)(128)(4,1)}), s8[4194304]{0:T(1024)(128)(4,1)S(1)}, s32[]{:S(2)}) async-start(s8[18939904]{0:T(1024)(128)(4,1)} %bitcast.30), calls=%async_computation.8 | async-start | bytes 8388608
  1355.3 26.0 %slice-start.1 = ((s8[18939904]{0:T(1024)(128)(4,1)}), s8[4194304]{0:T(1024)(128)(4,1)S(1)}, s32[]{:S(2)}) async-start(s8[18939904]{0:T(1024)(128)(4,1)} %bitcast.30), calls=%async_computation.9 | async-start | bytes 8388608
  1357.7 23.6 %slice-start.2 = ((s8[18939904]{0:T(1024)(128)(4,1)}), s8[4194304]{0:T(1024)(128)(4,1)S(1)}, s32[]{:S(2)}) async-start(s8[18939904]{0:T(1024)(128)(4,1)} %bitcast.30), calls=%async_computation.10 | async-start | bytes 8388608
  1357.7 23.6 %slice-start.3 = ((s8[18939904]{0:T(1024)(128)(4,1)}), s8[4194304]{0:T(1024)(128)(4,1)S(1)}, s32[]{:S(2)}) async-start(s8[18939904]{0:T(1024)(128)(4,1)} %bitcast.30), calls=%async_computation.11 | async-start | bytes 8388608
  1357.7 23.6 %slice-start.4 = ((s8[18939904]{0:T(1024)(128)(4,1)}), s8[2162688]{0:T(1024)(128)(4,1)S(1)}, s32[]{:S(2)}) async-start(s8[18939904]{0:T(1024)(128)(4,1)} %bitcast.30), calls=%async_computation.12 | async-start | bytes 4325376
Sparse Core Ops, SparseCore 0:
  916.8 64.2 all-gather.6
  984.6 101.6 all-gather.4
  1089.8 122.1 all-gather.10
  1215.4 122.3 all-gather.8
where the time goes:
time: 1400 us
  other arithmetic  607 us (43%)
  waiting for transfers between devices  507 us (36%)
  local copies, waits for them, and re-layouts  182 us (13%)
  blocking collectives  46.5 us (3%)
  starting transfers between devices  33.5 us (2%)
  between operations  19.9 us (1%)
    unnamed x5, other arithmetic  494 us
    all_gather x4, waiting for transfers between devices, lamb_tensor(): lax.all_gather(new_weight.astype(jnp.bfloat16), 'data', axis=1, tiled=True)  409 us
    unnamed x49, local copies, waits for them, and re-layouts  180 us
    all_to_all x4, waiting for transfers between devices, lamb_tensor(): received = lax.all_to_all(pieces, 'data', 1, 1, tiled=True)  97.2 us
    reduce_sum x4, other arithmetic, lamb_tensor(): grad_mean = jnp.sum(received, axis=1, dtype=jnp.float32) / groups  80.6 us
    psum x1, blocking collectives, lamb_tensor(): norm_pair = jnp.sqrt(lax.psum(part_sums, 'data'))  46.5 us
    all_to_all x4, starting transfers between devices, lamb_tensor(): received = lax.all_to_all(pieces, 'data', 1, 1, tiled=True)  33 us
  transfers between devices with their start and end apart: 8, of which 6 were waited for; matrix products, arithmetic and copies ran while one was open for 44% of the time, Pallas kernels for 0%

commit v1 on v0

v1 whole, which is shorter than its diff:
```python
import functools

import jax
import jax.numpy as jnp
from jax import lax
from jax.experimental import pallas as pl
from jax.experimental.pallas import tpu as pltpu
from jax.sharding import PartitionSpec as P

STEP = 10
LEARN_RATE = 0.1
BETA_ONE = 0.9
BETA_TWO = 0.999
EPSILON = 1e-6
WEIGHT_DECAY = 0.01

LANES = 128
ROWS = (867, 289, 1156, 1156)
PADDED = (880, 304, 1168, 1168)
STARTS = (0, 880, 1184, 2352)
TOTAL = 3520
UNITS = (
    (0, 0, 448, 0), (0, 448, 432, 1),
    (1, 0, 144, 0), (1, 144, 160, 1),
    (2, 0, 592, 0), (2, 592, 576, 1),
    (3, 0, 576, 0), (3, 576, 592, 1),
)
MAX_ROWS = 592
TILE = 48
MESH = pl.DeviceIdType.MESH
F32 = jnp.float32
BF16 = jnp.bfloat16


def pack_kernel(g0, g1, g2, g3, out):
    for t, ref in enumerate((g0, g1, g2, g3)):
        pad = jnp.zeros((PADDED[t] - ROWS[t], LANES), BF16)
        out[0, pl.ds(STARTS[t], PADDED[t]), :] = jnp.concatenate([ref[...].reshape(ROWS[t], LANES), pad], axis=0)


def pack(grads):
    specs = [pl.BlockSpec((1, r * LANES), lambda i: (0, i)) for r in ROWS]
    return pl.pallas_call(
        pack_kernel,
        grid=(32,),
        in_specs=specs,
        out_specs=pl.BlockSpec((1, TOTAL, LANES), lambda i: (i, 0, 0)),
        out_shape=jax.ShapeDtypeStruct((32, TOTAL, LANES), BF16),
        name="pack",
    )(*grads)


def unpack_kernel(full, w, m, v, c0, c1, c2, c3, *outs):
    for t, ref in enumerate((c0, c1, c2, c3)):
        ref[...] = full[0, pl.ds(STARTS[t], ROWS[t]), :].reshape(1, ROWS[t] * LANES)

    @pl.when(pl.program_id(0) == 0)
    def _():
        for s, src in enumerate((w, m, v)):
            for t in range(4):
                outs[4 * s + t][...] = src[pl.ds(STARTS[t], ROWS[t]), :].reshape(1, ROWS[t] * LANES)


def unpack(full, w, m, v):
    state = pl.BlockSpec((TOTAL, LANES), lambda i: (0, 0))
    return pl.pallas_call(
        unpack_kernel,
        grid=(32,),
        in_specs=[pl.BlockSpec((1, TOTAL, LANES), lambda i: (i, 0, 0)), state, state, state],
        out_specs=[pl.BlockSpec((1, r * LANES), lambda i: (0, i)) for r in ROWS]
        + [pl.BlockSpec((1, r * LANES), lambda i: (0, 0)) for r in ROWS] * 3,
        out_shape=[jax.ShapeDtypeStruct((1, 32 * r * LANES), BF16) for r in ROWS]
        + [jax.ShapeDtypeStruct((1, r * LANES), F32) for r in ROWS] * 3,
        name="unpack",
    )(full, w, m, v)


def comm_kernel(*refs):
    grads = refs[0]
    state_in = refs[1:13]
    full, new_w, new_m, new_v = refs[13:17]
    state = refs[17:29]
    (rx, r2, r3, rz, t2, lx, ns, nr, state_sem, lx_sem, p_send, p_recv, c_send, c_recv, q_send, q_recv,
     z_send, z_recv, n_send, n_recv, out_sem, own_sem, gz_send, gz_recv, gq_send, gq_recv, gp_send, gp_recv,
     gc_send, gc_recv) = refs[29:]

    me = lax.axis_index("data")
    c = me % 2
    x = (me // 2) % 2
    y = (me // 4) % 2
    z = me // 8

    def dev(zz, yy, xx, cc):
        return (((zz * 2 + yy) * 2 + xx) * 2 + cc,)

    core_peer = dev(z, y, x, 1 - c)
    x_peer = dev(z, y, 1 - x, c)
    y_peer = dev(z, 1 - y, x, c)
    z_peer = [dev((z + k) % 4, y, x, c) for k in (1, 2, 3)]

    barrier = pltpu.get_barrier_semaphore()
    for peer in [core_peer, x_peer, y_peer] + z_peer:
        pl.semaphore_signal(barrier, inc=1, device_id=peer, device_id_type=MESH)
    pl.semaphore_wait(barrier, 6)

    def remote(src, dst, ssem, rsem, peer):
        return pltpu.make_async_remote_copy(src_ref=src, dst_ref=dst, send_sem=ssem, recv_sem=rsem, device_id=peer, device_id_type=MESH)

    def rows_of(u):
        t, first, h, colour = UNITS[u]
        return pl.ds(STARTS[t] + first, h)

    def grad_slab(u, mine):
        rows = rows_of(u)
        if UNITS[u][3] == 0:
            return grads.at[:, :, x if mine else 1 - x, :, rows, :]
        return grads.at[:, y if mine else 1 - y, :, :, rows, :]

    def p_peer(u):
        return x_peer if UNITS[u][3] == 0 else y_peer

    def q_peer(u):
        return y_peer if UNITS[u][3] == 0 else x_peer

    def q_me(u):
        return y if UNITS[u][3] == 0 else x

    n_units = len(UNITS)
    p_copy = [remote(grad_slab(u, False), rx.at[:, :, :, rows_of(u), :], p_send.at[u], p_recv.at[u], p_peer(u)) for u in range(n_units)]
    lx_copy = [pltpu.make_async_copy(grad_slab(u, True), lx.at[u % 2, :, :, :, pl.ds(0, UNITS[u][2]), :], lx_sem.at[u % 2]) for u in range(n_units)]
    c_copy = [remote(t2.at[u % 2, :, :, pl.ds(0, UNITS[u][2]), :], r2.at[:, :, rows_of(u), :], c_send.at[u], c_recv.at[u], core_peer) for u in range(n_units)]
    q_copy = [remote(r2.at[:, 1 - q_me(u), rows_of(u), :], r3.at[:, rows_of(u), :], q_send.at[u], q_recv.at[u], q_peer(u)) for u in range(n_units)]
    z_copy = [[remote(r3.at[(z + k) % 4, rows_of(u), :], rz.at[k - 1, rows_of(u), :], z_send.at[u, k - 1], z_recv.at[u, k - 1], z_peer[k - 1]) for k in (1, 2, 3)] for u in range(n_units)]

    for u in range(n_units):
        p_copy[u].start()
    state_copy = [pltpu.make_async_copy(state_in[i], state[i], state_sem.at[i]) for i in range(12)]
    for cp in state_copy:
        cp.start()
    lx_copy[0].start()
    lx_copy[1].start()
    ns[...] = jnp.zeros_like(ns)

    def base(u):
        return STARTS[UNITS[u][0]] + UNITS[u][1]

    def core_step(u):
        lx_copy[u].wait()
        p_copy[u].wait_recv()
        if u >= 2:
            c_copy[u - 2].wait_send()

        def body(i, carry):
            r = pl.multiple_of(i * 16, 16)
            a = lx[u % 2, :, :, 1 - c, pl.ds(r, 16), :].astype(F32)
            b = rx[:, :, 1 - c, pl.ds(base(u) + r, 16), :].astype(F32)
            t2[u % 2, :, :, pl.ds(r, 16), :] = a + b
            return carry

        lax.fori_loop(0, UNITS[u][2] // 16, body, 0)
        c_copy[u].start()

    def q_step(u):
        c_copy[u].wait_recv()

        def body(i, carry):
            r = pl.multiple_of(i * 16, 16)
            a = lx[u % 2, :, :, c, pl.ds(r, 16), :].astype(F32)
            b = rx[:, :, c, pl.ds(base(u) + r, 16), :].astype(F32)
            r2[:, :, pl.ds(base(u) + r, 16), :] = r2[:, :, pl.ds(base(u) + r, 16), :] + (a + b)
            return carry

        lax.fori_loop(0, UNITS[u][2] // 16, body, 0)
        q_copy[u].start()
        if u + 2 < n_units:
            lx_copy[u + 2].start()

    def z_step(u):
        q_copy[u].wait_recv()

        def body(i, carry):
            r = pl.multiple_of(base(u) + i * 16, 16)
            r3[:, pl.ds(r, 16), :] = r3[:, pl.ds(r, 16), :] + r2[:, q_me(u), pl.ds(r, 16), :]
            return carry

        lax.fori_loop(0, UNITS[u][2] // 16, body, 0)
        for cp in z_copy[u]:
            cp.start()

    def lamb_step(u):
        t, first, h, colour = UNITS[u]
        for cp in z_copy[u]:
            cp.wait_recv()
        if u % 2 == 0:
            for i in (t, 4 + t, 8 + t):
                state_copy[i].wait()
        valid = min(h, ROWS[t] - first)
        q = q_me(u)

        def tile(r, n):
            rows = pl.ds(base(u) + r, n)
            flat = pl.ds((first + r) * LANES if isinstance(r, int) else pl.multiple_of((first + r) * LANES, LANES), n * LANES)
            w = state[t][:, flat].reshape(n, LANES)
            m = state[4 + t][:, flat].reshape(n, LANES)
            v = state[8 + t][:, flat].reshape(n, LANES)
            g = (((r3[z, rows, :] + rz[0, rows, :]) + rz[1, rows, :]) + rz[2, rows, :]) / 32.0
            nm = BETA_ONE * m + (1.0 - BETA_ONE) * g
            nv = BETA_TWO * v + (1.0 - BETA_TWO) * g * g
            u_dir = (nm / (1.0 - BETA_ONE ** STEP)) / (jnp.sqrt(nv / (1.0 - BETA_TWO ** STEP)) + EPSILON) + WEIGHT_DECAY * w
            r2[0, q, rows, :] = nm
            r2[1, q, rows, :] = nv
            rz[0, rows, :] = u_dir
            return w * w, u_dir * u_dir

        def body(i, carry):
            ww, uu = tile(pl.multiple_of(i * TILE, 16), TILE)
            return (carry[0] + jnp.sum(ww.reshape(TILE // 8, 8, LANES), axis=0), carry[1] + jnp.sum(uu.reshape(TILE // 8, 8, LANES), axis=0))

        zero = jnp.zeros((8, LANES), F32)
        acc_w, acc_u = lax.fori_loop(0, valid // TILE, body, (zero, zero))
        sum_w = jnp.sum(acc_w, axis=0, keepdims=True)
        sum_u = jnp.sum(acc_u, axis=0, keepdims=True)
        if valid % TILE:
            ww, uu = tile(valid - valid % TILE, valid % TILE)
            sum_w = sum_w + jnp.sum(ww, axis=0, keepdims=True)
            sum_u = sum_u + jnp.sum(uu, axis=0, keepdims=True)
        ns[pl.ds(2 * t, 1), :] = ns[pl.ds(2 * t, 1), :] + sum_w
        ns[pl.ds(2 * t + 1, 1), :] = ns[pl.ds(2 * t + 1, 1), :] + sum_u
        out_m[u].start()
        out_v[u].start()

    out_m = [pltpu.make_async_copy(r2.at[0, q_me(u), rows_of(u), :], new_m.at[rows_of(u), :], out_sem.at[0, u]) for u in range(n_units)]
    out_v = [pltpu.make_async_copy(r2.at[1, q_me(u), rows_of(u), :], new_v.at[rows_of(u), :], out_sem.at[1, u]) for u in range(n_units)]
    out_w = [pltpu.make_async_copy(rz.at[1, rows_of(u), :], new_w.at[rows_of(u), :], out_sem.at[2, u]) for u in range(n_units)]
    own_copy = [pltpu.make_async_copy(rx.at[0, 0, 0, rows_of(u), :], full.at[z, y, x, c, rows_of(u), :], own_sem.at[u]) for u in range(n_units)]

    for s in range(n_units + 3):
        if s < n_units:
            core_step(s)
        if 0 <= s - 1 < n_units:
            q_step(s - 1)
        if 0 <= s - 2 < n_units:
            z_step(s - 2)
        if 0 <= s - 3 < n_units:
            lamb_step(s - 3)

    for i, peer in enumerate((core_peer, x_peer, y_peer)):
        cp = remote(ns, nr.at[i], n_send.at[i], n_recv.at[i], peer)
        cp.start()
        cp.wait()
        ns[...] = ns[...] + nr[i]
    z_norm = [remote(ns, nr.at[3 + z], n_send.at[2 + k], n_recv.at[2 + k], z_peer[k - 1]) for k in (1, 2, 3)]
    for cp in z_norm:
        cp.start()
    nr[3 + z] = ns[...]
    for k in (1, 2, 3):
        remote(ns, nr.at[3 + (z + 4 - k) % 4], n_send.at[2 + k], n_recv.at[2 + k], z_peer[k - 1]).wait_recv()
    for cp in z_norm:
        cp.wait_send()
    total = (nr[3] + nr[4]) + (nr[5] + nr[6])
    norms = jnp.sqrt(jnp.sum(total, axis=1, keepdims=True))

    def weight_step(u):
        t, first, h, colour = UNITS[u]
        valid = min(h, ROWS[t] - first)
        scale = LEARN_RATE * (norms[2 * t:2 * t + 1] / norms[2 * t + 1:2 * t + 2])

        def tile(r, n):
            rows = pl.ds(base(u) + r, n)
            flat = pl.ds((first + r) * LANES if isinstance(r, int) else pl.multiple_of((first + r) * LANES, LANES), n * LANES)
            w = state[t][:, flat].reshape(n, LANES)
            nw = w - scale * rz[0, rows, :]
            rz[1, rows, :] = nw
            rx[0, 0, 0, rows, :] = nw.astype(BF16)

        def body(i, carry):
            tile(pl.multiple_of(i * TILE, 16), TILE)
            return carry

        lax.fori_loop(0, valid // TILE, body, 0)
        if valid % TILE:
            tile(valid - valid % TILE, valid % TILE)
        own_copy[u].start()
        out_w[u].start()

    def slab(u, zz, yy, xx, cc):
        return full.at[zz, yy, xx, cc, rows_of(u), :]

    def gathered_q(u):
        return full.at[:, y, x, c, rows_of(u), :]

    def gathered_p(u):
        if UNITS[u][3] == 0:
            return full.at[:, :, x, c, rows_of(u), :]
        return full.at[:, y, :, c, rows_of(u), :]

    def gathered_c(u):
        return full.at[:, :, :, c, rows_of(u), :]

    gz = [[remote(slab(u, z, y, x, c), slab(u, z, y, x, c), gz_send.at[u, k - 1], gz_recv.at[u, k - 1], z_peer[k - 1]) for k in (1, 2, 3)] for u in range(n_units)]
    gq = [remote(gathered_q(u), gathered_q(u), gq_send.at[u], gq_recv.at[u], q_peer(u)) for u in range(n_units)]
    gp = [remote(gathered_p(u), gathered_p(u), gp_send.at[u], gp_recv.at[u], p_peer(u)) for u in range(n_units)]
    gc = [remote(gathered_c(u), gathered_c(u), gc_send.at[u], gc_recv.at[u], core_peer) for u in range(n_units)]

    for s in range(n_units + 4):
        if s < n_units:
            weight_step(s)
            own_copy[s].wait()
            for cp in gz[s]:
                cp.start()
        if 0 <= s - 1 < n_units:
            for cp in gz[s - 1]:
                cp.wait_recv()
            gq[s - 1].start()
        if 0 <= s - 2 < n_units:
            gq[s - 2].wait_recv()
            gp[s - 2].start()
        if 0 <= s - 3 < n_units:
            gp[s - 3].wait_recv()
            gc[s - 3].start()
        if 0 <= s - 4 < n_units:
            gc[s - 4].wait_recv()

    for u in range(n_units):
        p_copy[u].wait_send()
        if u >= n_units - 2:
            c_copy[u].wait_send()
        q_copy[u].wait_send()
        for cp in z_copy[u] + gz[u]:
            cp.wait_send()
        gq[u].wait_send()
        gp[u].wait_send()
        gc[u].wait_send()
        out_m[u].wait()
        out_v[u].wait()
        out_w[u].wait()


def comm(grads, state):
    n_units = len(UNITS)
    any_spec = pl.BlockSpec(memory_space=pl.ANY)
    dma = pltpu.SemaphoreType.DMA
    return pl.pallas_call(
        comm_kernel,
        in_specs=[any_spec] * 13,
        out_specs=[any_spec] * 4,
        out_shape=[jax.ShapeDtypeStruct((4, 2, 2, 2, TOTAL, LANES), BF16)] + [jax.ShapeDtypeStruct((TOTAL, LANES), F32)] * 3,
        scratch_shapes=[pltpu.VMEM((1, r * LANES), F32) for r in ROWS] * 3
        + [
            pltpu.VMEM((4, 2, 2, TOTAL, LANES), BF16),
            pltpu.VMEM((4, 2, TOTAL, LANES), F32),
            pltpu.VMEM((4, TOTAL, LANES), F32),
            pltpu.VMEM((3, TOTAL, LANES), F32),
            pltpu.VMEM((2, 4, 2, MAX_ROWS, LANES), F32),
            pltpu.VMEM((2, 4, 2, 2, MAX_ROWS, LANES), BF16),
            pltpu.VMEM((8, LANES), F32),
            pltpu.VMEM((7, 8, LANES), F32),
            dma((12,)), dma((2,)),
            dma((n_units,)), dma((n_units,)), dma((n_units,)), dma((n_units,)), dma((n_units,)), dma((n_units,)),
            dma((n_units, 3)), dma((n_units, 3)), dma((6,)), dma((6,)), dma((3, n_units)), dma((n_units,)),
            dma((n_units, 3)), dma((n_units, 3)), dma((n_units,)), dma((n_units,)), dma((n_units,)), dma((n_units,)),
            dma((n_units,)), dma((n_units,)),
        ],
        compiler_params=pltpu.CompilerParams(collective_id=0, has_side_effects=True, vmem_limit_bytes=64 * 1024 * 1024 - 128 * 1024),
        name="lamb_comm",
    )(grads, *state)


def solution(mesh):
    grad_spec = P("data", None, None)
    shard_spec = P(None, "data")
    full_spec = P(None, None)

    def device_step(*blocks):
        grads = pack([blocks[4 * t].reshape(1, -1) for t in range(4)])
        state = [blocks[4 * t + s] for s in (1, 2, 3) for t in range(4)]
        full, w, m, v = comm(grads.reshape(4, 2, 2, 2, TOTAL, LANES), state)
        outs = unpack(full.reshape(32, TOTAL, LANES), w, m, v)
        results = []
        for t in range(4):
            results.extend((outs[t], outs[4 + t], outs[8 + t], outs[12 + t]))
        return tuple(results)

    return jax.shard_map(device_step, mesh=mesh, in_specs=(grad_spec, shard_spec, shard_spec, shard_spec) * 4, out_specs=(full_spec, shard_spec, shard_spec, shard_spec) * 4, check_vma=False)
```

time: 1400 us -> 646 us (0.46)
  the two profiles are of different devices: /device:TPU:0 before, /device:TPU:25 now
where the time goes in v1:
time: 646 us; the launch traced here: 645 us
  Pallas kernels  644 us (100%)
    pallas_call x1, Pallas kernels, comm(): pl.pallas_call(comm_kernel, in_specs=[any_spec] * 13, out_specs=[any_spec...  542 us
    pallas_call x1, Pallas kernels, unpack(): pl.pallas_call(unpack_kernel, grid=(32,), in_specs=[pl.BlockSpec((1, TOTA...  65.1 us
    pallas_call x1, Pallas kernels, pack(): pl.pallas_call(pack_kernel, grid=(32,), in_specs=specs, out_specs=pl.Bloc...  37.4 us

profile of v1, /device:TPU:25, one launch (start us, length us, event | category | flops | bytes accessed | tf_op | source)
XLA Modules:
  0.0 645.0 jit_solution(17181225597219321579)
XLA Ops:
  0.6 37.4 %pack.1 = bf16[32,3520,128]{2,1,0:T(8,128)(2,1)} custom-call(bf16[1,3551232]{1,0:T(2,128)(2,1)} %bitcast.10, bf16[1,1183744]{1,0:T(2,128)(2,1)} %bitcast.11, bf16[1,4734976]{1,0:T(2,128)(2,1)} %bitcast.8, bf16[1,4734976]{1,0:T(2,128)(2,1)} %bitcast.9), custom_call_target="tpu_custom_call" | custom-call | tf_op jit(solution)/shard_map/pack/pallas_call | solution.py:43
  38.1 541.9 %lamb_comm.1 = (bf16[4,2,2,2,3520,128]{5,4,3,2,1,0:T(8,128)(2,1)}, f32[3520,128]{1,0:T(8,128)}, f32[3520,128]{1,0:T(8,128)}, f32[3520,128]{1,0:T(8,128)}) custom-call(bf16[4,2,2,2,3520,128]{5,4,3,2,1,0:T(8,128)(2,1)} %bitcast.6, f32[1,110976]{1,0:T(1,128)} %refs_1_.1, f32[1,36992]{1,0:T(1,128)} %refs_2_.1, f32[1,147968]{1,0:T(1,128)} %refs_3_.1, ...), custom_call_target="tpu_custom_call" | custom-call | tf_op jit(solution)/shard_map/lamb_comm/pallas_call | solution.py:343
  579.9 65.1 %unpack.1 = (bf16[1,3551232]{1,0:T(2,128)(2,1)}, bf16[1,1183744]{1,0:T(2,128)(2,1)}, bf16[1,4734976]{1,0:T(2,128)(2,1)}, bf16[1,4734976]{1,0:T(2,128)(2,1)}, f32...) custom-call(bf16[32,3520,128]{2,1,0:T(8,128)(2,1)} %bitcast.7, ...), custom_call_target="tpu_custom_call" | custom-call | tf_op jit(solution)/shard_map/unpack/pallas_call | solution.py:66

commit v2 on v1

v2 whole, which is shorter than its diff:
```python
import functools

import jax
import jax.numpy as jnp
from jax import lax
from jax.experimental import pallas as pl
from jax.experimental.pallas import tpu as pltpu
from jax.sharding import PartitionSpec as P

STEP = 10
LEARN_RATE = 0.1
BETA_ONE = 0.9
BETA_TWO = 0.999
EPSILON = 1e-6
WEIGHT_DECAY = 0.01

LANES = 128
ROWS = (867, 289, 1156, 1156)
PADDED = (880, 304, 1168, 1168)
STARTS = (0, 880, 1184, 2352)
TOTAL = 3520
STEPS = (
    ((2, 0, 304), (2, 304, 288)),
    ((2, 592, 288), (2, 880, 288)),
    ((3, 0, 288), (3, 288, 304)),
    ((3, 592, 288), (3, 880, 288)),
    ((0, 0, 224), (0, 224, 224)),
    ((0, 448, 224), (0, 672, 208)),
    ((1, 0, 80), (1, 80, 80)),
    ((1, 160, 80), (1, 240, 64)),
)
UNITS = tuple(unit + (colour,) for step in STEPS for colour, unit in enumerate(step))
MAX_ROWS = 304
TILE = 48
MESH = pl.DeviceIdType.MESH
F32 = jnp.float32
BF16 = jnp.bfloat16


def unpack_kernel(full, w, m, v, c0, c1, c2, c3, *outs):
    for t, ref in enumerate((c0, c1, c2, c3)):
        ref[...] = full[0, pl.ds(STARTS[t], ROWS[t]), :].astype(F32).reshape(1, ROWS[t] * LANES).astype(BF16)

    @pl.when(pl.program_id(0) == 0)
    def _():
        for s, src in enumerate((w, m, v)):
            for t in range(4):
                outs[4 * s + t][...] = src[pl.ds(STARTS[t], ROWS[t]), :].reshape(1, ROWS[t] * LANES)


def unpack(full, w, m, v):
    state = pl.BlockSpec((TOTAL, LANES), lambda i: (0, 0))
    return pl.pallas_call(
        unpack_kernel,
        grid=(32,),
        in_specs=[pl.BlockSpec((1, TOTAL, LANES), lambda i: (i, 0, 0)), state, state, state],
        out_specs=[pl.BlockSpec((1, r * LANES), lambda i: (0, i)) for r in ROWS]
        + [pl.BlockSpec((1, r * LANES), lambda i: (0, 0)) for r in ROWS] * 3,
        out_shape=[jax.ShapeDtypeStruct((1, 32 * r * LANES), BF16) for r in ROWS]
        + [jax.ShapeDtypeStruct((1, r * LANES), F32) for r in ROWS] * 3,
        name="unpack",
    )(full, w, m, v)


def comm_kernel(*refs):
    grads = refs[0:4]
    state_in = refs[4:16]
    full, new_w, new_m, new_v = refs[16:20]
    state = refs[20:32]
    (rx, r2, r3, rz, t2, lx, ps, stage, ns, nr, state_sem, stage_sem, p_send, p_recv, c_send, c_recv, q_send, q_recv,
     z_send, z_recv, n_send, n_recv, out_sem, own_sem, gz_send, gz_recv, gq_send, gq_recv, gp_send, gp_recv,
     gc_send, gc_recv) = refs[32:]

    me = lax.axis_index("data")
    c = me % 2
    x = (me // 2) % 2
    y = (me // 4) % 2
    z = me // 8

    def dev(zz, yy, xx, cc):
        return (((zz * 2 + yy) * 2 + xx) * 2 + cc,)

    def flip(value, by):
        return 1 - value if by else value

    core_peer = dev(z, y, x, 1 - c)
    x_peer = dev(z, y, 1 - x, c)
    y_peer = dev(z, 1 - y, x, c)
    z_peer = [dev((z + k) % 4, y, x, c) for k in (1, 2, 3)]
    plane_peer = [dev(z, flip(y, k // 4), flip(x, k // 2 % 2), flip(c, k % 2)) for k in range(1, 8)]
    plane_slot = [flip(y, k // 4) * 4 + flip(x, k // 2 % 2) * 2 + flip(c, k % 2) for k in range(8)]

    barrier = pltpu.get_barrier_semaphore()
    for peer in plane_peer + z_peer:
        pl.semaphore_signal(barrier, inc=1, device_id=peer, device_id_type=MESH)

    def remote(src, dst, ssem, rsem, peer):
        return pltpu.make_async_remote_copy(src_ref=src, dst_ref=dst, send_sem=ssem, recv_sem=rsem, device_id=peer, device_id_type=MESH)

    n_units = len(UNITS)
    n_steps = len(STEPS)
    units = range(n_units)

    def base(u):
        return STARTS[UNITS[u][0]] + UNITS[u][1]

    def rows_of(u):
        return pl.ds(base(u), UNITS[u][2])

    def valid_of(u):
        return min(UNITS[u][2], ROWS[UNITS[u][0]] - UNITS[u][1])

    def p_peer(u):
        return x_peer if UNITS[u][3] == 0 else y_peer

    def q_peer(u):
        return y_peer if UNITS[u][3] == 0 else x_peer

    def q_me(u):
        return y if UNITS[u][3] == 0 else x

    def stage_copy(u, mine):
        t, first, h, colour = UNITS[u]
        lanes = pl.ds(first * LANES, valid_of(u) * LANES)
        if colour == 0:
            src = grads[t].at[:, :, x if mine else 1 - x, :, :, lanes]
        else:
            src = grads[t].at[:, y if mine else 1 - y, :, :, :, lanes]
        return pltpu.make_async_copy(src, stage.at[colour, :, :, :, :, pl.ds(0, valid_of(u) * LANES)], stage_sem.at[colour])

    def pack(u, store):
        h, colour = UNITS[u][2:]
        valid = valid_of(u)

        def body(j, carry):
            for cc in (0, 1):
                dense = stage[colour, j // 2, j % 2, cc, :, pl.ds(0, valid * LANES)].reshape(valid, LANES)
                if valid < h:
                    dense = jnp.concatenate([dense, jnp.zeros((h - valid, LANES), BF16)], axis=0)
                store(j // 2, j % 2, cc, dense)
            return carry

        lax.fori_loop(0, 8, body, 0)

    def pack_send(u):
        h, colour = UNITS[u][2:]

        def store(zz, qq, cc, dense):
            ps[colour, (u // 2) % 2, zz, qq, cc, pl.ds(0, h), :] = dense

        pack(u, store)

    def pack_own(u):
        h, colour = UNITS[u][2:]

        def store(zz, qq, cc, dense):
            lx[colour, zz, qq, cc, pl.ds(0, h), :] = dense

        pack(u, store)

    p_copy = [remote(ps.at[u % 2, (u // 2) % 2, :, :, :, pl.ds(0, UNITS[u][2]), :], rx.at[:, :, :, rows_of(u), :], p_send.at[u], p_recv.at[u], p_peer(u)) for u in units]
    c_copy = [remote(t2.at[u % 2, :, :, pl.ds(0, UNITS[u][2]), :], r2.at[:, :, rows_of(u), :], c_send.at[u], c_recv.at[u], core_peer) for u in units]
    q_copy = [remote(r2.at[:, 1 - q_me(u), rows_of(u), :], r3.at[:, rows_of(u), :], q_send.at[u], q_recv.at[u], q_peer(u)) for u in units]
    z_copy = [[remote(r3.at[(z + k) % 4, rows_of(u), :], rz.at[k - 1, rows_of(u), :], z_send.at[u, k - 1], z_recv.at[u, k - 1], z_peer[k - 1]) for k in (1, 2, 3)] for u in units]
    out_m = [pltpu.make_async_copy(r2.at[0, q_me(u), rows_of(u), :], new_m.at[rows_of(u), :], out_sem.at[0, u]) for u in units]
    out_v = [pltpu.make_async_copy(r2.at[1, q_me(u), rows_of(u), :], new_v.at[rows_of(u), :], out_sem.at[1, u]) for u in units]
    out_w = [pltpu.make_async_copy(rz.at[1, rows_of(u), :], new_w.at[rows_of(u), :], out_sem.at[2, u]) for u in units]
    own_copy = [pltpu.make_async_copy(rx.at[0, 0, 0, rows_of(u), :], full.at[z, y, x, c, rows_of(u), :], own_sem.at[u]) for u in units]
    state_copy = [pltpu.make_async_copy(state_in[i], state[i], state_sem.at[i]) for i in range(12)]

    def core_step(u):
        with jax.named_scope(f"wait_p#u={u}"):
            p_copy[u].wait_recv()
        if u >= 2:
            c_copy[u - 2].wait_send()

        def body(i, carry):
            r = pl.multiple_of(i * 16, 16)
            a = lx[u % 2, :, :, 1 - c, pl.ds(r, 16), :].astype(F32)
            b = rx[:, :, 1 - c, pl.ds(base(u) + r, 16), :].astype(F32)
            t2[u % 2, :, :, pl.ds(r, 16), :] = a + b
            return carry

        lax.fori_loop(0, UNITS[u][2] // 16, body, 0)
        c_copy[u].start()

    def q_step(u):
        with jax.named_scope(f"wait_c#u={u}"):
            c_copy[u].wait_recv()

        def body(i, carry):
            r = pl.multiple_of(i * 16, 16)
            a = lx[u % 2, :, :, c, pl.ds(r, 16), :].astype(F32)
            b = rx[:, :, c, pl.ds(base(u) + r, 16), :].astype(F32)
            r2[:, :, pl.ds(base(u) + r, 16), :] = r2[:, :, pl.ds(base(u) + r, 16), :] + (a + b)
            return carry

        lax.fori_loop(0, UNITS[u][2] // 16, body, 0)
        q_copy[u].start()

    def z_step(u):
        with jax.named_scope(f"wait_q#u={u}"):
            q_copy[u].wait_recv()

        def body(i, carry):
            r = pl.multiple_of(base(u) + i * 16, 16)
            r3[:, pl.ds(r, 16), :] = r3[:, pl.ds(r, 16), :] + r2[:, q_me(u), pl.ds(r, 16), :]
            return carry

        lax.fori_loop(0, UNITS[u][2] // 16, body, 0)
        for cp in z_copy[u]:
            cp.start()

    def flat_rows(u, r, n):
        start = (UNITS[u][1] + r) * LANES
        return pl.ds(start if isinstance(r, int) else pl.multiple_of(start, LANES), n * LANES)

    def lamb_step(u):
        t, first, h, colour = UNITS[u]
        with jax.named_scope(f"wait_z#u={u}"):
            for cp in z_copy[u]:
                cp.wait_recv()
        if first == 0:
            for i in (t, 4 + t, 8 + t):
                state_copy[i].wait()
        valid = valid_of(u)
        q = q_me(u)

        def tile(r, n):
            rows = pl.ds(base(u) + r, n)
            flat = flat_rows(u, r, n)
            w = state[t][:, flat].reshape(n, LANES)
            m = state[4 + t][:, flat].reshape(n, LANES)
            v = state[8 + t][:, flat].reshape(n, LANES)
            g = (((r3[z, rows, :] + rz[0, rows, :]) + rz[1, rows, :]) + rz[2, rows, :]) / 32.0
            nm = BETA_ONE * m + (1.0 - BETA_ONE) * g
            nv = BETA_TWO * v + (1.0 - BETA_TWO) * g * g
            u_dir = (nm / (1.0 - BETA_ONE ** STEP)) / (jnp.sqrt(nv / (1.0 - BETA_TWO ** STEP)) + EPSILON) + WEIGHT_DECAY * w
            r2[0, q, rows, :] = nm
            r2[1, q, rows, :] = nv
            rz[0, rows, :] = u_dir
            return w * w, u_dir * u_dir

        def body(i, carry):
            ww, uu = tile(pl.multiple_of(i * TILE, 16), TILE)
            return (carry[0] + jnp.sum(ww.reshape(TILE // 8, 8, LANES), axis=0), carry[1] + jnp.sum(uu.reshape(TILE // 8, 8, LANES), axis=0))

        zero = jnp.zeros((8, LANES), F32)
        acc_w, acc_u = lax.fori_loop(0, valid // TILE, body, (zero, zero))
        sum_w = jnp.sum(acc_w, axis=0, keepdims=True)
        sum_u = jnp.sum(acc_u, axis=0, keepdims=True)
        if valid % TILE:
            ww, uu = tile(valid - valid % TILE, valid % TILE)
            sum_w = sum_w + jnp.sum(ww, axis=0, keepdims=True)
            sum_u = sum_u + jnp.sum(uu, axis=0, keepdims=True)
        ns[pl.ds(2 * t, 1), :] = ns[pl.ds(2 * t, 1), :] + sum_w
        ns[pl.ds(2 * t + 1, 1), :] = ns[pl.ds(2 * t + 1, 1), :] + sum_u
        out_m[u].start()
        out_v[u].start()

    def pair(s):
        return (2 * s, 2 * s + 1)

    for s in (0, 1):
        for u in pair(s):
            stage_copy(u, False).start()
        if s == 0:
            for cp in state_copy:
                cp.start()
            ns[...] = jnp.zeros_like(ns)
        for u in pair(s):
            stage_copy(u, False).wait()
            pack_send(u)
        if s == 0:
            pl.semaphore_wait(barrier, 10)
        for u in pair(s):
            p_copy[u].start()
    for u in pair(0):
        stage_copy(u, True).start()
    for u in pair(0):
        stage_copy(u, True).wait()
        pack_own(u)
        stage_copy(u + 4, False).start()

    for s in range(n_steps + 2):
        if s < n_steps:
            for u in pair(s):
                core_step(u)
            for u in pair(s):
                q_step(u)
            if s + 2 < n_steps:
                for u in pair(s + 2):
                    stage_copy(u, False).wait()
                    p_copy[u - 4].wait_send()
                    pack_send(u)
                    p_copy[u].start()
            if s + 1 < n_steps:
                for u in pair(s + 1):
                    stage_copy(u, True).start()
                for u in pair(s + 1):
                    stage_copy(u, True).wait()
                    pack_own(u)
                    if s + 3 < n_steps:
                        stage_copy(u + 4, False).start()
        if 0 <= s - 1 < n_steps:
            for u in pair(s - 1):
                z_step(u)
        if 0 <= s - 2 < n_steps:
            for u in pair(s - 2):
                lamb_step(u)

    with jax.named_scope("norms"):
        plane_norm = [remote(ns, nr.at[plane_slot[0]], n_send.at[k], n_recv.at[plane_slot[0]], plane_peer[k - 1]) for k in range(1, 8)]
        for cp in plane_norm:
            cp.start()
        nr[plane_slot[0]] = ns[...]
        for k in range(1, 8):
            remote(ns, nr.at[plane_slot[k]], n_send.at[k], n_recv.at[plane_slot[k]], plane_peer[k - 1]).wait_recv()
        for cp in plane_norm:
            cp.wait_send()
        ns[...] = ((nr[0] + nr[1]) + (nr[2] + nr[3])) + ((nr[4] + nr[5]) + (nr[6] + nr[7]))
        z_norm = [remote(ns, nr.at[8 + z], n_send.at[7 + k], n_recv.at[8 + z], z_peer[k - 1]) for k in (1, 2, 3)]
        for cp in z_norm:
            cp.start()
        nr[8 + z] = ns[...]
        for k in (1, 2, 3):
            zz = (z + k) % 4
            remote(ns, nr.at[8 + zz], n_send.at[7 + k], n_recv.at[8 + zz], z_peer[k - 1]).wait_recv()
        for cp in z_norm:
            cp.wait_send()
    total = (nr[8] + nr[9]) + (nr[10] + nr[11])
    norms = jnp.sqrt(jnp.sum(total, axis=1, keepdims=True))

    def gathered_q(u):
        return full.at[:, y, x, c, rows_of(u), :]

    def gathered_p(u):
        if UNITS[u][3] == 0:
            return full.at[:, :, x, c, rows_of(u), :]
        return full.at[:, y, :, c, rows_of(u), :]

    def gathered_c(u):
        return full.at[:, :, :, c, rows_of(u), :]

    gz = [[remote(rx.at[0, 0, 0, rows_of(u), :], full.at[z, y, x, c, rows_of(u), :], gz_send.at[u, k - 1], gz_recv.at[u, k - 1], z_peer[k - 1]) for k in (1, 2, 3)] for u in units]
    gq = [remote(gathered_q(u), gathered_q(u), gq_send.at[u], gq_recv.at[u], q_peer(u)) for u in units]
    gp = [remote(gathered_p(u), gathered_p(u), gp_send.at[u], gp_recv.at[u], p_peer(u)) for u in units]
    gc = [remote(gathered_c(u), gathered_c(u), gc_send.at[u], gc_recv.at[u], core_peer) for u in units]

    def weight_step(u):
        t = UNITS[u][0]
        valid = valid_of(u)
        scale = LEARN_RATE * (norms[2 * t:2 * t + 1] / norms[2 * t + 1:2 * t + 2])

        def tile(r, n):
            rows = pl.ds(base(u) + r, n)
            w = state[t][:, flat_rows(u, r, n)].reshape(n, LANES)
            nw = w - scale * rz[0, rows, :]
            rz[1, rows, :] = nw
            rx[0, 0, 0, rows, :] = nw.astype(BF16)

        def body(i, carry):
            tile(pl.multiple_of(i * TILE, 16), TILE)
            return carry

        lax.fori_loop(0, valid // TILE, body, 0)
        if valid % TILE:
            tile(valid - valid % TILE, valid % TILE)
        own_copy[u].start()
        for cp in gz[u]:
            cp.start()
        out_w[u].start()

    order = list(range(n_steps))[::-1]
    for i in (0, 1):
        for u in pair(order[i]):
            weight_step(u)
    for i in range(n_steps + 3):
        if i < n_steps:
            for u in pair(order[i]):
                own_copy[u].wait()
                with jax.named_scope(f"wait_gz#u={u}"):
                    for cp in gz[u]:
                        cp.wait_recv()
                gq[u].start()
        if i + 2 < n_steps:
            for u in pair(order[i + 2]):
                weight_step(u)
        if 0 <= i - 1 < n_steps:
            for u in pair(order[i - 1]):
                with jax.named_scope(f"wait_gq#u={u}"):
                    gq[u].wait_recv()
                gp[u].start()
        if 0 <= i - 2 < n_steps:
            for u in pair(order[i - 2]):
                with jax.named_scope(f"wait_gp#u={u}"):
                    gp[u].wait_recv()
                gc[u].start()
        if 0 <= i - 3 < n_steps:
            for u in pair(order[i - 3]):
                with jax.named_scope(f"wait_gc#u={u}"):
                    gc[u].wait_recv()

    for u in units:
        if u >= n_units - 4:
            p_copy[u].wait_send()
        if u >= n_units - 2:
            c_copy[u].wait_send()
        q_copy[u].wait_send()
        for cp in z_copy[u] + gz[u]:
            cp.wait_send()
        gq[u].wait_send()
        gp[u].wait_send()
        gc[u].wait_send()
        out_m[u].wait()
        out_v[u].wait()
        out_w[u].wait()


def comm(grads, state):
    n_units = len(UNITS)
    any_spec = pl.BlockSpec(memory_space=pl.ANY)
    dma = pltpu.SemaphoreType.DMA
    return pl.pallas_call(
        comm_kernel,
        in_specs=[any_spec] * 16,
        out_specs=[any_spec] * 4,
        out_shape=[jax.ShapeDtypeStruct((4, 2, 2, 2, TOTAL, LANES), BF16)] + [jax.ShapeDtypeStruct((TOTAL, LANES), F32)] * 3,
        scratch_shapes=[pltpu.VMEM((1, r * LANES), F32) for r in ROWS] * 3
        + [
            pltpu.VMEM((4, 2, 2, TOTAL, LANES), BF16),
            pltpu.VMEM((4, 2, TOTAL, LANES), F32),
            pltpu.VMEM((4, TOTAL, LANES), F32),
            pltpu.VMEM((3, TOTAL, LANES), F32),
            pltpu.VMEM((2, 4, 2, MAX_ROWS, LANES), F32),
            pltpu.VMEM((2, 4, 2, 2, MAX_ROWS, LANES), BF16),
            pltpu.VMEM((2, 2, 4, 2, 2, MAX_ROWS, LANES), BF16),
            pltpu.VMEM((2, 4, 2, 2, 1, MAX_ROWS * LANES), BF16),
            pltpu.VMEM((8, LANES), F32),
            pltpu.VMEM((12, 8, LANES), F32),
            dma((12,)), dma((2,)),
            dma((n_units,)), dma((n_units,)), dma((n_units,)), dma((n_units,)), dma((n_units,)), dma((n_units,)),
            dma((n_units, 3)), dma((n_units, 3)), dma((11,)), dma((12,)), dma((3, n_units)), dma((n_units,)),
            dma((n_units, 3)), dma((n_units, 3)), dma((n_units,)), dma((n_units,)), dma((n_units,)), dma((n_units,)),
            dma((n_units,)), dma((n_units,)),
        ],
        compiler_params=pltpu.CompilerParams(collective_id=0, has_side_effects=True, vmem_limit_bytes=64 * 1024 * 1024 - 128 * 1024),
        name="lamb_comm",
    )(*grads, *state)


def solution(mesh):
    grad_spec = P("data", None, None)
    shard_spec = P(None, "data")
    full_spec = P(None, None)

    def device_step(*blocks):
        grads = [blocks[4 * t].reshape(4, 2, 2, 2, 1, -1) for t in range(4)]
        state = [blocks[4 * t + s] for s in (1, 2, 3) for t in range(4)]
        full, w, m, v = comm(grads, state)
        outs = unpack(full.reshape(32, TOTAL, LANES), w, m, v)
        results = []
        for t in range(4):
            results.extend((outs[t], outs[4 + t], outs[8 + t], outs[12 + t]))
        return tuple(results)

    return jax.shard_map(device_step, mesh=mesh, in_specs=(grad_spec, shard_spec, shard_spec, shard_spec) * 4, out_specs=(full_spec, shard_spec, shard_spec, shard_spec) * 4, check_vma=False)
```

time: 646 us -> 481 us (0.74)
  the two profiles are of different devices: /device:TPU:25 before, /device:TPU:0 now
where the time goes in v2:
time: 481 us; the launch traced here: 478 us
  Pallas kernels  477 us (99%)
    pallas_call x1, Pallas kernels, comm(): pl.pallas_call(comm_kernel, in_specs=[any_spec] * 16, out_specs=[any_spec...  420 us
    pallas_call x1, Pallas kernels, unpack(): pl.pallas_call(unpack_kernel, grid=(32,), in_specs=[pl.BlockSpec((1, TOTA...  57 us

profile of v2, /device:TPU:0, one launch (start us, length us, event | category | flops | bytes accessed | tf_op | source)
XLA Modules:
  0.0 477.7 jit_solution(4537128636452298869)
XLA Ops:
  0.7 420.0 %lamb_comm.1 = (bf16[4,2,2,2,3520,128]{5,4,3,2,1,0:T(8,128)(2,1)}, f32[3520,128]{1,0:T(8,128)}, f32[3520,128]{1,0:T(8,128)}, f32[3520,128]{1,0:T(8,128)}) custom-call(bf16[4,2,2,2,1,110976]{5,4,3,2,1,0:T(2,128)(2,1)} %bitcast.8, bf16[4,2,2,2,1,36992]{5,4,3,2,1,0:T(2,128)(2,1)} %bitcast.9, bf16[4,2,2,2,1,147968]{5,4,3,2,1,0:T(2,128)(2,1)} %bitcast.6, ...), custom_call_target="tpu_custom_call" | custom-call | tf_op jit(solution)/shard_map/lamb_comm/pallas_call | solution.py:424
  420.7 57.0 %unpack.1 = (bf16[1,3551232]{1,0:T(2,128)(2,1)}, bf16[1,1183744]{1,0:T(2,128)(2,1)}, bf16[1,4734976]{1,0:T(2,128)(2,1)}, bf16[1,4734976]{1,0:T(2,128)(2,1)}, f32...) custom-call(bf16[32,3520,128]{2,1,0:T(8,128)(2,1)} %bitcast.5, ...), custom_call_target="tpu_custom_call" | custom-call | tf_op jit(solution)/shard_map/unpack/pallas_call | solution.py:53

commit v3 on v2

--- a/solution.py
+++ b/solution.py
@@ -20,17 +20,20 @@
 STARTS = (0, 880, 1184, 2352)
 TOTAL = 3520
 STEPS = (
-    ((2, 0, 304), (2, 304, 288)),
-    ((2, 592, 288), (2, 880, 288)),
-    ((3, 0, 288), (3, 288, 304)),
-    ((3, 592, 288), (3, 880, 288)),
+    ((2, 0, 192), (2, 192, 176)),
+    ((2, 368, 176), (2, 544, 192)),
+    ((3, 0, 192), (3, 192, 192)),
+    ((3, 384, 192), (3, 576, 192)),
+    ((3, 768, 192), (3, 960, 208)),
     ((0, 0, 224), (0, 224, 224)),
     ((0, 448, 224), (0, 672, 208)),
     ((1, 0, 80), (1, 80, 80)),
     ((1, 160, 80), (1, 240, 64)),
 )
-UNITS = tuple(unit + (colour,) for step in STEPS for colour, unit in enumerate(step))
-MAX_ROWS = 304
+THIRD = ((2, 736, 208, 2), (2, 944, 224, 2))
+UNITS = tuple(unit + (colour,) for step in STEPS for colour, unit in enumerate(step)) + THIRD
+MAX_ROWS = 224
+LAG = 4
 TILE = 48
 MESH = pl.DeviceIdType.MESH
 F32 = jnp.float32
@@ -67,7 +70,7 @@
     state_in = refs[4:16]
     full, new_w, new_m, new_v = refs[16:20]
     state = refs[20:32]
-    (rx, r2, r3, rz, t2, lx, ps, stage, ns, nr, state_sem, stage_sem, p_send, p_recv, c_send, c_recv, q_send, q_recv,
+    (rx, r2, r3, rz, t2, lx, ps, stage, rx3, t23, ps3, ns, nr, state_sem, stage_sem, p_send, p_recv, c_send, c_recv, q_send, q_recv,
      z_send, z_recv, n_send, n_recv, out_sem, own_sem, gz_send, gz_recv, gq_send, gq_recv, gp_send, gp_recv,
      gc_send, gc_recv) = refs[32:]
 
@@ -118,6 +121,9 @@
 
     def q_me(u):
         return y if UNITS[u][3] == 0 else x
+
+    third = [2 * n_steps + i for i in range(len(THIRD))]
+    pair_units = range(2 * n_steps)
 
     def stage_copy(u, mine):
         t, first, h, colour = UNITS[u]
@@ -158,10 +164,10 @@
 
         pack(u, store)
 
-    p_copy = [remote(ps.at[u % 2, (u // 2) % 2, :, :, :, pl.ds(0, UNITS[u][2]), :], rx.at[:, :, :, rows_of(u), :], p_send.at[u], p_recv.at[u], p_peer(u)) for u in units]
-    c_copy = [remote(t2.at[u % 2, :, :, pl.ds(0, UNITS[u][2]), :], r2.at[:, :, rows_of(u), :], c_send.at[u], c_recv.at[u], core_peer) for u in units]
-    q_copy = [remote(r2.at[:, 1 - q_me(u), rows_of(u), :], r3.at[:, rows_of(u), :], q_send.at[u], q_recv.at[u], q_peer(u)) for u in units]
-    z_copy = [[remote(r3.at[(z + k) % 4, rows_of(u), :], rz.at[k - 1, rows_of(u), :], z_send.at[u, k - 1], z_recv.at[u, k - 1], z_peer[k - 1]) for k in (1, 2, 3)] for u in units]
+    p_copy = [remote(ps.at[u % 2, (u // 2) % 2, :, :, :, pl.ds(0, UNITS[u][2]), :], rx.at[:, :, :, rows_of(u), :], p_send.at[u], p_recv.at[u], p_peer(u)) for u in pair_units]
+    c_copy = [remote(t2.at[u % 2, :, :, pl.ds(0, UNITS[u][2]), :], r2.at[:, :, rows_of(u), :], c_send.at[u], c_recv.at[u], core_peer) for u in pair_units]
+    q_copy = [remote(r2.at[:, 1 - q_me(u), rows_of(u), :], r3.at[:, rows_of(u), :], q_send.at[u], q_recv.at[u], q_peer(u)) for u in pair_units]
+    z_copy = [[remote(r3.at[(z + k) % 4, rows_of(u), :], rz.at[k - 1, rows_of(u), :], z_send.at[u, k - 1], z_recv.at[u, k - 1], z_peer[k - 1]) for k in (1, 2, 3)] for u in pair_units]
     out_m = [pltpu.make_async_copy(r2.at[0, q_me(u), rows_of(u), :], new_m.at[rows_of(u), :], out_sem.at[0, u]) for u in units]
     out_v = [pltpu.make_async_copy(r2.at[1, q_me(u), rows_of(u), :], new_v.at[rows_of(u), :], out_sem.at[1, u]) for u in units]
     out_w = [pltpu.make_async_copy(rz.at[1, rows_of(u), :], new_w.at[rows_of(u), :], out_sem.at[2, u]) for u in units]
@@ -211,6 +217,85 @@
         for cp in z_copy[u]:
             cp.start()
 
+    def third_parts(u):
+        i, h = u - 2 * n_steps, UNITS[u][2]
+        rows = rows_of(u)
+        short = pl.ds(0, h)
+        landing = [rx.at[0:2, :, :, rows, :], rx.at[2:4, :, :, rows, :], rx3.at[i, :, :, :, short, :]]
+        first = [remote(ps3.at[i, (z + k) % 4, :, :, :, short, :], landing[k - 1], z_send.at[u, k - 1], z_recv.at[u, k - 1], z_peer[k - 1]) for k in (1, 2, 3)]
+        core = remote(t23.at[i, :, :, short, :], r2.at[0:2, :, rows, :], c_send.at[u], c_recv.at[u], core_peer)
+        along_x = remote(r2.at[0:2, 1 - x, rows, :], r3.at[0:2, rows, :], q_send.at[u], q_recv.at[u], x_peer)
+        along_y = remote(r3.at[1 - y, rows, :], rz.at[0, rows, :], p_send.at[u], p_recv.at[u], y_peer)
+        return first, core, along_x, along_y
+
+    third_copy = {u: third_parts(u) for u in third}
+
+    def third_stage(u):
+        t, first, h, colour = UNITS[u]
+        valid = valid_of(u)
+        lanes = pl.ds(first * LANES, valid * LANES)
+        copies = [pltpu.make_async_copy(grads[t].at[:, :, :, cc, :, lanes], stage.at[cc, :, :, :, :, pl.ds(0, valid * LANES)], stage_sem.at[cc]) for cc in (0, 1)]
+        for cp in copies:
+            cp.start()
+        for cp in copies:
+            cp.wait()
+
+        def body(j, carry):
+            for xx in (0, 1):
+                for cc in (0, 1):
+                    dense = stage[cc, j // 2, j % 2, xx, :, pl.ds(0, valid * LANES)].reshape(valid, LANES)
+                    if valid < h:
+                        dense = jnp.concatenate([dense, jnp.zeros((h - valid, LANES), BF16)], axis=0)
+                    ps3[u - 2 * n_steps, j // 2, j % 2, xx, cc, pl.ds(0, h), :] = dense
+            return carry
+
+        lax.fori_loop(0, 8, body, 0)
+        for cp in third_copy[u][0]:
+            cp.start()
+
+    def third_sum(u, r, cc):
+        i = u - 2 * n_steps
+        near = pl.ds(base(u) + r, 16)
+        own = ps3[i, z, :, :, cc, pl.ds(r, 16), :].astype(F32) + rx[0:2, :, cc, near, :].astype(F32)
+        return own + (rx[2:4, :, cc, near, :].astype(F32) + rx3[i, :, :, cc, pl.ds(r, 16), :].astype(F32))
+
+    def third_core_step(u):
+        with jax.named_scope(f"wait_third_z#u={u}"):
+            for cp in third_copy[u][0]:
+                cp.wait_recv()
+
+        def body(i, carry):
+            r = pl.multiple_of(i * 16, 16)
+            t23[u - 2 * n_steps, :, :, pl.ds(r, 16), :] = third_sum(u, r, 1 - c)
+            return carry
+
+        lax.fori_loop(0, UNITS[u][2] // 16, body, 0)
+        third_copy[u][1].start()
+
+    def third_x_step(u):
+        third_copy[u][1].wait_recv()
+
+        def body(i, carry):
+            r = pl.multiple_of(i * 16, 16)
+            near = pl.ds(base(u) + r, 16)
+            r2[0:2, :, near, :] = r2[0:2, :, near, :] + third_sum(u, r, c)
+            return carry
+
+        lax.fori_loop(0, UNITS[u][2] // 16, body, 0)
+        third_copy[u][2].start()
+
+    def third_y_step(u):
+        with jax.named_scope(f"wait_third_x#u={u}"):
+            third_copy[u][2].wait_recv()
+
+        def body(i, carry):
+            near = pl.ds(pl.multiple_of(base(u) + i * 16, 16), 16)
+            r3[0:2, near, :] = r3[0:2, near, :] + r2[0:2, x, near, :]
+            return carry
+
+        lax.fori_loop(0, UNITS[u][2] // 16, body, 0)
+        third_copy[u][3].start()
+
     def flat_rows(u, r, n):
         start = (UNITS[u][1] + r) * LANES
         return pl.ds(start if isinstance(r, int) else pl.multiple_of(start, LANES), n * LANES)
@@ -218,8 +303,11 @@
     def lamb_step(u):
         t, first, h, colour = UNITS[u]
         with jax.named_scope(f"wait_z#u={u}"):
-            for cp in z_copy[u]:
-                cp.wait_recv()
+            if colour == 2:
+                third_copy[u][3].wait_recv()
+            else:
+                for cp in z_copy[u]:
+                    cp.wait_recv()
         if first == 0:
             for i in (t, 4 + t, 8 + t):
                 state_copy[i].wait()
@@ -232,7 +320,10 @@
             w = state[t][:, flat].reshape(n, LANES)
             m = state[4 + t][:, flat].reshape(n, LANES)
             v = state[8 + t][:, flat].reshape(n, LANES)
-            g = (((r3[z, rows, :] + rz[0, rows, :]) + rz[1, rows, :]) + rz[2, rows, :]) / 32.0
+            if colour == 2:
+                g = (r3[y, rows, :] + rz[0, rows, :]) / 32.0
+            else:
+                g = (((r3[z, rows, :] + rz[0, rows, :]) + rz[1, rows, :]) + rz[2, rows, :]) / 32.0
             nm = BETA_ONE * m + (1.0 - BETA_ONE) * g
             nv = BETA_TWO * v + (1.0 - BETA_TWO) * g * g
             u_dir = (nm / (1.0 - BETA_ONE ** STEP)) / (jnp.sqrt(nv / (1.0 - BETA_TWO ** STEP)) + EPSILON) + WEIGHT_DECAY * w
@@ -275,6 +366,7 @@
             pl.semaphore_wait(barrier, 10)
         for u in pair(s):
             p_copy[u].start()
+        third_stage(third[s])
     for u in pair(0):
         stage_copy(u, True).start()
     for u in pair(0):
@@ -282,12 +374,20 @@
         pack_own(u)
         stage_copy(u + 4, False).start()
 
-    for s in range(n_steps + 2):
+    for s in range(n_steps + LAG):
         if s < n_steps:
             for u in pair(s):
                 core_step(u)
             for u in pair(s):
                 q_step(u)
+            if s == 4:
+                for u in third:
+                    third_core_step(u)
+            if s == n_steps - 2:
+                third_x_step(third[0])
+            if s == n_steps - 1:
+                third_x_step(third[1])
+                third_y_step(third[0])
             if s + 2 < n_steps:
                 for u in pair(s + 2):
                     stage_copy(u, False).wait()
@@ -305,9 +405,13 @@
         if 0 <= s - 1 < n_steps:
             for u in pair(s - 1):
                 z_step(u)
-        if 0 <= s - 2 < n_steps:
-            for u in pair(s - 2):
+        if s == n_steps:
+            third_y_step(third[1])
+        if 0 <= s - LAG < n_steps:
+            for u in pair(s - LAG):
                 lamb_step(u)
+    for u in third:
+        lamb_step(u)
 
     with jax.named_scope("norms"):
         plane_norm = [remote(ns, nr.at[plane_slot[0]], n_send.at[k], n_recv.at[plane_slot[0]], plane_peer[k - 1]) for k in range(1, 8)]
@@ -332,19 +436,30 @@
     norms = jnp.sqrt(jnp.sum(total, axis=1, keepdims=True))
 
     def gathered_q(u):
+        if UNITS[u][3] == 2:
+            return full.at[z, y, x, c, rows_of(u), :]
         return full.at[:, y, x, c, rows_of(u), :]
 
     def gathered_p(u):
         if UNITS[u][3] == 0:
             return full.at[:, :, x, c, rows_of(u), :]
+        if UNITS[u][3] == 2:
+            return full.at[z, :, x, c, rows_of(u), :]
         return full.at[:, y, :, c, rows_of(u), :]
 
     def gathered_c(u):
         return full.at[:, :, :, c, rows_of(u), :]
 
-    gz = [[remote(rx.at[0, 0, 0, rows_of(u), :], full.at[z, y, x, c, rows_of(u), :], gz_send.at[u, k - 1], gz_recv.at[u, k - 1], z_peer[k - 1]) for k in (1, 2, 3)] for u in units]
-    gq = [remote(gathered_q(u), gathered_q(u), gq_send.at[u], gq_recv.at[u], q_peer(u)) for u in units]
-    gp = [remote(gathered_p(u), gathered_p(u), gp_send.at[u], gp_recv.at[u], p_peer(u)) for u in units]
+    def gather_z(u, k):
+        src = rx.at[0, 0, 0, rows_of(u), :]
+        dst = full.at[z, y, x, c, rows_of(u), :]
+        if UNITS[u][3] == 2:
+            src = dst = full.at[z, :, :, c, rows_of(u), :]
+        return remote(src, dst, gz_send.at[u, k - 1], gz_recv.at[u, k - 1], z_peer[k - 1])
+
+    gz = [[gather_z(u, k) for k in (1, 2, 3)] for u in units]
+    gq = [remote(gathered_q(u), gathered_q(u), gq_send.at[u], gq_recv.at[u], y_peer if UNITS[u][3] == 2 else q_peer(u)) for u in units]
+    gp = [remote(gathered_p(u), gathered_p(u), gp_send.at[u], gp_recv.at[u], x_peer if UNITS[u][3] == 2 else p_peer(u)) for u in units]
     gc = [remote(gathered_c(u), gathered_c(u), gc_send.at[u], gc_recv.at[u], core_peer) for u in units]
 
     def weight_step(u):
@@ -367,14 +482,33 @@
         if valid % TILE:
             tile(valid - valid % TILE, valid % TILE)
         own_copy[u].start()
+        out_w[u].start()
+        if UNITS[u][3] == 2:
+            own_copy[u].wait()
+            gq[u].start()
+        else:
+            for cp in gz[u]:
+                cp.start()
+
+    def third_gather_z(u):
+        with jax.named_scope(f"wait_third_gx#u={u}"):
+            gp[u].wait_recv()
         for cp in gz[u]:
             cp.start()
-        out_w[u].start()
+
+    def third_gather_core(u):
+        with jax.named_scope(f"wait_third_gz#u={u}"):
+            for cp in gz[u]:
+                cp.wait_recv()
+        gc[u].start()
 
     order = list(range(n_steps))[::-1]
-    for i in (0, 1):
-        for u in pair(order[i]):
-            weight_step(u)
+    for u in pair(order[0]):
+        weight_step(u)
+    for u in third:
+        weight_step(u)
+    for u in pair(order[1]):
+        weight_step(u)
     for i in range(n_steps + 3):
         if i < n_steps:
             for u in pair(order[i]):
@@ -383,31 +517,51 @@
                     for cp in gz[u]:
                         cp.wait_recv()
                 gq[u].start()
+        if i == 0:
+            for u in third:
+                gq[u].wait_recv()
+                gp[u].start()
         if i + 2 < n_steps:
             for u in pair(order[i + 2]):
                 weight_step(u)
+        if i == 3:
+            third_gather_z(third[0])
+        if i == n_steps - 3:
+            third_gather_z(third[1])
         if 0 <= i - 1 < n_steps:
             for u in pair(order[i - 1]):
                 with jax.named_scope(f"wait_gq#u={u}"):
                     gq[u].wait_recv()
                 gp[u].start()
+        if i == n_steps - 1:
+            third_gather_core(third[0])
         if 0 <= i - 2 < n_steps:
             for u in pair(order[i - 2]):
                 with jax.named_scope(f"wait_gp#u={u}"):
                     gp[u].wait_recv()
                 gc[u].start()
+        if i == n_steps + 1:
+            third_gather_core(third[1])
         if 0 <= i - 3 < n_steps:
             for u in pair(order[i - 3]):
                 with jax.named_scope(f"wait_gc#u={u}"):
                     gc[u].wait_recv()
-
-    for u in units:
-        if u >= n_units - 4:
+    for u in third:
+        gc[u].wait_recv()
+
+    for u in pair_units:
+        if u >= 2 * n_steps - 4:
             p_copy[u].wait_send()
-        if u >= n_units - 2:
+        if u >= 2 * n_steps - 2:
             c_copy[u].wait_send()
         q_copy[u].wait_send()
-        for cp in z_copy[u] + gz[u]:
+        for cp in z_copy[u]:
+            cp.wait_send()
+    for u in third:
+        for cp in third_copy[u][0] + list(third_copy[u][1:]):
+            cp.wait_send()
+    for u in units:
+        for cp in gz[u]:
             cp.wait_send()
         gq[u].wait_send()
         gp[u].wait_send()
@@ -436,6 +590,9 @@
             pltpu.VMEM((2, 4, 2, 2, MAX_ROWS, LANES), BF16),
             pltpu.VMEM((2, 2, 4, 2, 2, MAX_ROWS, LANES), BF16),
             pltpu.VMEM((2, 4, 2, 2, 1, MAX_ROWS * LANES), BF16),
+            pltpu.VMEM((2, 2, 2, 2, MAX_ROWS, LANES), BF16),
+            pltpu.VMEM((2, 2, 2, MAX_ROWS, LANES), F32),
+            pltpu.VMEM((2, 4, 2, 2, 2, MAX_ROWS, LANES), BF16),
             pltpu.VMEM((8, LANES), F32),
             pltpu.VMEM((12, 8, LANES), F32),
             dma((12,)), dma((2,)),

time: 481 us -> 433 us (0.900)
  Pallas kernels: 477 us -> 430 us
    pallas_call x1, Pallas kernels: 420 us -> 373 us  [comm(): pl.pallas_call(comm_kernel, in_specs=[any_spec] * 16, out_specs=[any_spec...]
where the time goes in v3:
time: 433 us; the launch traced here: 431 us
  Pallas kernels  430 us (99%)
    pallas_call x1, Pallas kernels, comm(): pl.pallas_call(comm_kernel, in_specs=[any_spec] * 16, out_specs=[any_spec...  373 us
    pallas_call x1, Pallas kernels, unpack(): pl.pallas_call(unpack_kernel, grid=(32,), in_specs=[pl.BlockSpec((1, TOTA...  57 us

profile of v3, /device:TPU:0, one launch (start us, length us, event | category | flops | bytes accessed | tf_op | source)
XLA Modules:
  0.0 431.0 jit_solution(7699071028744590443)
XLA Ops:
  0.7 373.4 %lamb_comm.1 = (bf16[4,2,2,2,3520,128]{5,4,3,2,1,0:T(8,128)(2,1)}, f32[3520,128]{1,0:T(8,128)}, f32[3520,128]{1,0:T(8,128)}, f32[3520,128]{1,0:T(8,128)}) custom-call(bf16[4,2,2,2,1,110976]{5,4,3,2,1,0:T(2,128)(2,1)} %bitcast.8, bf16[4,2,2,2,1,36992]{5,4,3,2,1,0:T(2,128)(2,1)} %bitcast.9, bf16[4,2,2,2,1,147968]{5,4,3,2,1,0:T(2,128)(2,1)} %bitcast.6, ...), custom_call_target="tpu_custom_call" | custom-call | tf_op jit(solution)/shard_map/lamb_comm/pallas_call | solution.py:578
  374.0 57.0 %unpack.1 = (bf16[1,3551232]{1,0:T(2,128)(2,1)}, bf16[1,1183744]{1,0:T(2,128)(2,1)}, bf16[1,4734976]{1,0:T(2,128)(2,1)}, bf16[1,4734976]{1,0:T(2,128)(2,1)}, f32...) custom-call(bf16[32,3520,128]{2,1,0:T(8,128)(2,1)} %bitcast.5, ...), custom_call_target="tpu_custom_call" | custom-call | tf_op jit(solution)/shard_map/unpack/pallas_call | solution.py:56
